TPU v7x, 32 devices: a whole 2x2x4 slice. The times are simulated.
32 devices in a mesh: dap: 8 (over y, x, core), hc: 4 (over z).
Axes of the slice: x: 2, y: 2, z: 4, core: 2. Of those that a mesh axis runs over, the one named last changes fastest.
Arguments:
- alignment: bfloat16 [64, 512, 256], P('dap'), may hold values from -6 to 6
- align_mask: int32 [64, 512], P('dap'), may hold values 0 or 1
- residue_mask: int32 [512], replicated, may hold values 0 or 1
- chain_index: int32 [512], replicated, may hold values from 0 to 7, never falling along the last dimension, each value on 1 to 256 neighbouring positions
- pair_input: bfloat16 [512, 512, 128], P('dap', 'hc'), may hold values from -6 to 6
- offset_table: bfloat16 [66, 128], replicated, may hold values from -6 to 6
- bias_weight: bfloat16 [128, 8], replicated, may hold values from -16 to 16
- query_weight: bfloat16 [256, 256], P(None, 'hc'), may hold values from -0.375 to 0.375
- key_weight: bfloat16 [256, 256], P(None, 'hc'), may hold values from -0.375 to 0.375
- value_weight: bfloat16 [256, 256], P(None, 'hc'), may hold values from -0.375 to 0.375
- gate_weight: bfloat16 [256, 256], P(None, 'hc'), may hold values from -0.375 to 0.375
- output_weight: bfloat16 [256, 256], replicated, may hold values from -0.375 to 0.375
- left_gate_weight: bfloat16 [128, 128], replicated, may hold values from -0.5 to 0.5
- left_weight: bfloat16 [128, 128], replicated, may hold values from -0.5 to 0.5
- right_gate_weight: bfloat16 [128, 128], replicated, may hold values from -0.5 to 0.5
- right_weight: bfloat16 [128, 128], replicated, may hold values from -0.5 to 0.5
- update_gate_weight: bfloat16 [128, 128], replicated, may hold values from -0.5 to 0.5
- update_out_weight: bfloat16 [128, 128], replicated, may hold values from -0.5 to 0.5
Outputs:
- alignment_out: bfloat16 [64, 512, 256], P('dap')
- pair_out: bfloat16 [512, 512, 128], P('dap', 'hc')
All inputs are finite; a program needn't handle non-finite values. No bound on the sum of `align_mask` on one device may be relied on, other than what follows from the above.
Results may differ from a plain program's by a relative error of at most 0.0079.
Values may be sent and summed in bfloat16 or wider, within the bound.
A program may use at most 128 MiB of HBM per device.

v0:
```python
import jax
import jax.numpy as jnp
from jax import lax
from jax.sharding import PartitionSpec as P

HEAD_DIM = 32
REACH = 32


EPSILON = 1e-05
MASKED = 1000000000.0


def normalize(values, along):
    values = values.astype(jnp.float32)
    average = jnp.mean(values, axis=along, keepdims=True)
    centred = values - average
    variance = jnp.mean(centred * centred, axis=along, keepdims=True)
    return centred * lax.rsqrt(variance + EPSILON)


def project(inputs, weight, pattern):
    return jnp.einsum(pattern, inputs, weight, preferred_element_type=jnp.float32)


def unscramble(blocked, dap_size, hc_size, row_count, col_count):
    channels = blocked.shape[0]
    arranged = blocked.reshape(channels, dap_size, hc_size, row_count, col_count)
    arranged = jnp.transpose(arranged, (0, 1, 3, 2, 4))
    return arranged.reshape(channels, dap_size * row_count, hc_size * col_count)


def scramble(blocked, dap_size, hc_size, row_count, col_count):
    channels = blocked.shape[0]
    arranged = blocked.reshape(channels, dap_size, row_count, hc_size, col_count)
    arranged = jnp.transpose(arranged, (0, 1, 3, 2, 4))
    return arranged.reshape(channels, dap_size * hc_size * row_count, col_count)


def on_device(
    alignment,
    align_mask,
    residue_mask,
    chain_index,
    pair_input,
    offset_table,
    bias_weight,
    query_weight,
    key_weight,
    value_weight,
    gate_weight,
    output_weight,
    left_gate_weight,
    left_weight,
    right_gate_weight,
    right_weight,
    update_gate_weight,
    update_out_weight,
):
    row_count = pair_input.shape[0]
    col_count = pair_input.shape[1]
    residues = residue_mask.shape[0]
    dap_size = lax.axis_size("dap")
    hc_size = lax.axis_size("hc")
    row_first = lax.axis_index("dap") * row_count
    col_first = lax.axis_index("hc") * col_count
    row_ids = row_first + jnp.arange(row_count, dtype=jnp.int32)
    col_ids = col_first + jnp.arange(col_count, dtype=jnp.int32)
    row_chain = lax.dynamic_slice_in_dim(chain_index, row_first, row_count, 0)
    col_chain = lax.dynamic_slice_in_dim(chain_index, col_first, col_count, 0)
    offsets = jnp.clip(row_ids[:, None] - col_ids[None, :] + REACH, 0, 2 * REACH)
    bin_index = jnp.where(row_chain[:, None] == col_chain[None, :], offsets, 2 * REACH + 1)
    slot_count = 128
    one_hot = (
        bin_index[:, :, None] == jnp.arange(slot_count, dtype=jnp.int32)[None, None, :]
    ).astype(jnp.bfloat16)
    padded_table = jnp.pad(offset_table, ((0, slot_count - offset_table.shape[0]), (0, 0)))
    pair_state = pair_input.astype(jnp.float32) + project(one_hot, padded_table, "ijb,bc->ijc")
    pair_norm = normalize(pair_state, 2).astype(jnp.bfloat16)
    head_bias = project(pair_norm, bias_weight, "ijc,ch->ihj")
    head_bias = lax.all_to_all(head_bias, "hc", split_axis=1, concat_axis=2, tiled=True)
    align_norm = normalize(alignment, 2).astype(jnp.bfloat16)
    scaling = HEAD_DIM ** (-0.5)
    queries = (project(align_norm, query_weight, "snc,ce->sen") * scaling).astype(jnp.bfloat16)
    keys_all = project(align_norm, key_weight, "snc,ce->sen").astype(jnp.bfloat16)
    values_all = project(align_norm, value_weight, "snc,ce->sen").astype(jnp.bfloat16)
    gates_all = project(align_norm, gate_weight, "snc,ce->sen").astype(jnp.bfloat16)
    key_bias = MASKED * ((align_mask * residue_mask[None, :]).astype(jnp.float32) - 1.0)
    local_heads = query_weight.shape[1] // HEAD_DIM
    bias_rows = lax.all_gather(head_bias, "dap", axis=0, tiled=True)
    row_span = bias_rows.shape[0]
    bias_heads = jnp.transpose(bias_rows, (1, 0, 2))

    def per_sequence(members):
        query_seq, keys_seq, values_seq, gates_seq, masking = members
        query_rows = query_seq.reshape(local_heads, HEAD_DIM, row_span)
        gate_rows = gates_seq.reshape(local_heads, HEAD_DIM, row_span)
        keys_heads = keys_seq.reshape(local_heads, HEAD_DIM, residues)
        values_heads = values_seq.reshape(local_heads, HEAD_DIM, residues)
        scores = jnp.einsum(
            "hdi,hdj->hij", query_rows, keys_heads, preferred_element_type=jnp.float32
        )
        scores = scores + bias_heads + masking[None, None, :]
        weights = jax.nn.softmax(scores, axis=-1).astype(jnp.bfloat16)
        mixed = jnp.einsum(
            "hij,hdj->hdi", weights, values_heads, preferred_element_type=jnp.float32
        )
        mixed = mixed * jax.nn.sigmoid(gate_rows.astype(jnp.float32))
        return mixed.astype(jnp.bfloat16).reshape(local_heads * HEAD_DIM, row_span)

    attended = lax.map(per_sequence, (queries, keys_all, values_all, gates_all, key_bias))
    merged = project(
        lax.all_gather(attended, "hc", axis=1, tiled=True), output_weight, "sen,ec->snc"
    )
    alignment_out = (alignment.astype(jnp.float32) + merged).astype(jnp.bfloat16)
    residue_rows = lax.dynamic_slice_in_dim(residue_mask, row_first, row_count, 0)
    residue_cols = lax.dynamic_slice_in_dim(residue_mask, col_first, col_count, 0)
    pair_mask = (residue_rows[:, None] * residue_cols[None, :]).astype(jnp.float32)
    update_gate = jax.nn.sigmoid(project(pair_norm, update_gate_weight, "ijc,ce->ije"))
    left_side = jax.nn.sigmoid(project(pair_norm, left_gate_weight, "ijc,ce->eij")) * project(
        pair_norm, left_weight, "ijc,ce->eij"
    )
    left_side = (left_side * pair_mask[None, :, :]).astype(jnp.bfloat16)
    right_side = jax.nn.sigmoid(project(pair_norm, right_gate_weight, "ijc,ce->eij")) * project(
        pair_norm, right_weight, "ijc,ce->eij"
    )
    right_side = (right_side * pair_mask[None, :, :]).astype(jnp.bfloat16)
    joint_left, joint_right = (
        lax.all_to_all(left_side, ("dap", "hc"), split_axis=0, concat_axis=1, tiled=True),
        lax.all_to_all(right_side, ("dap", "hc"), split_axis=0, concat_axis=1, tiled=True),
    )
    left_all = unscramble(joint_left, dap_size, hc_size, row_count, col_count)
    right_all = unscramble(joint_right, dap_size, hc_size, row_count, col_count)
    triangle = jnp.einsum(
        "cik,cjk->cij", left_all, right_all, preferred_element_type=jnp.float32
    ).astype(jnp.bfloat16)
    triangle_local = lax.all_to_all(
        scramble(triangle, dap_size, hc_size, row_count, col_count),
        ("dap", "hc"),
        split_axis=1,
        concat_axis=0,
        tiled=True,
    )
    triangle_norm = normalize(triangle_local, 0).astype(jnp.bfloat16)
    update = project(triangle_norm, update_out_weight, "eij,ec->ijc") * update_gate
    pair_out = (pair_state + update).astype(jnp.bfloat16)
    return (alignment_out, pair_out)


def solution(mesh):
    placed = (
        P("dap", None, None),
        P("dap", None),
        P(),
        P(),
        P("dap", "hc", None),
        P(),
        P(),
        P(None, "hc"),
        P(None, "hc"),
        P(None, "hc"),
        P(None, "hc"),
        P(),
        P(),
        P(),
        P(),
        P(),
        P(),
        P(),
    )
    return jax.shard_map(
        on_device,
        mesh=mesh,
        in_specs=placed,
        out_specs=(P("dap", None, None), P("dap", "hc", None)),
        check_vma=False,
    )
```

profile of v0, /device:TPU:0, one launch (start us, length us, event | category | flops | bytes accessed | tf_op | source)
XLA Modules:
  0.0 282.8 jit_solution(12638223589419799453)
XLA Ops:
  8.8 3.2 %copy.116 = bf16[64,128,128]{1,2,0:T(8,128)(2,1)S(1)} copy(bf16[64,128,128]{2,1,0:T(8,128)(2,1)} %param.24) | data formatting | bytes 4194304 | tf_op args[4]
  18.0 6.3 %all-to-all-start = ((f32[64,8,128]{2,0,1:T(8,128)}), f32[64,8,128]{2,0,1:T(8,128)S(1)}, u32[]{:S(2)}, u32[]{:S(2)}) async-start(f32[64,8,128]{2,0,1:T(8,128)} %copy.119), calls=%async_computation | async-start | bytes 524288 | tf_op jit(solution)/shard_map/all_to_all | solution.py:81
  26.8 2.7 copy.133
  29.5 3.7 %all-to-all-done = f32[64,8,128]{2,0,1:T(8,128)S(1)} async-done(((f32[64,8,128]{2,0,1:T(8,128)}), f32[64,8,128]{2,0,1:T(8,128)S(1)}, u32[]{:S(2)}, u32[]{:S(2)}) %all-to-all-start) | async-done | bytes 262176 | tf_op jit(solution)/shard_map/all_to_all | solution.py:81
  33.2 3.8 %all-to-all-start.2 = ((bf16[128,64,128]{2,1,0:T(8,128)(2,1)}), bf16[128,64,128]{2,1,0:T(8,128)(2,1)}, u32[]{:S(2)}, u32[]{:S(2)}) async-start(bf16[128,64,128]{2,1,0:T(8,128)(2,1)} %copy.133), calls=%async_computation.2 | async-start | bytes 4194304 | tf_op jit(solution)/shard_map/all_to_all | solution.py:130
  39.4 2.7 copy.126
  42.0 41.9 %all-to-all-done.2 = bf16[128,64,128]{2,1,0:T(8,128)(2,1)} async-done(((bf16[128,64,128]{2,1,0:T(8,128)(2,1)}), bf16[128,64,128]{2,1,0:T(8,128)(2,1)}, u32[]{:S(2)}, u32[]{:S(2)}) %all-to-all-start.2) | async-done | bytes 2097184 | tf_op jit(solution)/shard_map/all_to_all | solution.py:130
  83.9 4.7 %all-to-all-start.1 = ((bf16[128,64,128]{2,1,0:T(8,128)(2,1)}), bf16[128,64,128]{2,1,0:T(8,128)(2,1)}, u32[]{:S(2)}, u32[]{:S(2)}) async-start(bf16[128,64,128]{2,1,0:T(8,128)(2,1)} %copy.126), calls=%async_computation.1 | async-start | bytes 4194304 | tf_op jit(solution)/shard_map/all_to_all | solution.py:129
  94.2 2.3 fusion.19
  98.1 2.3 fusion.21
  100.4 3.6 %copy.135 = bf16[4,8,64,4,128]{4,3,2,1,0:T(4,128)(2,1)S(1)} copy(bf16[4,8,64,4,128]{4,2,0,3,1:T(8,128)(2,1)} %bitcast.36) | data formatting | bytes 4194304 | tf_op jit(solution)/shard_map/transpose | solution.py:29
  104.0 2.2 reshape.188
  106.2 29.1 %all-to-all-done.1 = bf16[128,64,128]{2,1,0:T(8,128)(2,1)} async-done(((bf16[128,64,128]{2,1,0:T(8,128)(2,1)}), bf16[128,64,128]{2,1,0:T(8,128)(2,1)}, u32[]{:S(2)}, u32[]{:S(2)}) %all-to-all-start.1) | async-done | bytes 2097184 | tf_op jit(solution)/shard_map/all_to_all | solution.py:129
  135.3 3.6 %copy.128 = bf16[4,8,64,4,128]{4,3,2,1,0:T(4,128)(2,1)S(1)} copy(bf16[4,8,64,4,128]{4,2,0,3,1:T(8,128)(2,1)} %bitcast.28) | data formatting | bytes 4194304 | tf_op jit(solution)/shard_map/transpose | solution.py:29
  138.8 2.2 reshape.186
  141.0 4.9 %convolution_convert_fusion = bf16[4,512,512]{2,1,0:T(8,128)(2,1)} fusion(bf16[4,512,512]{2,1,0:T(8,128)(2,1)} %reshape.186, bf16[4,512,512]{2,1,0:T(8,128)(2,1)} %reshape.188), kind=kOutput, calls=%fused_computation.38 | convolution fusion | flops 1074790400 | bytes 6291456 | tf_op jit(solution)/shard_map/cik,cjk->cij/dot_general | solution.py:134
  145.9 2.5 reshape.189
  149.0 10.9 %copy.137 = bf16[4,2048,128]{2,0,1:T(4,128)(2,1)} copy(bf16[4,2048,128]{2,1,0:T(8,128)(2,1)S(1)} %bitcast.137) | data formatting | bytes 4194304 | tf_op jit(solution)/shard_map/reshape | solution.py:37
  159.9 5.0 %all-to-all-start.3 = ((bf16[4,2048,128]{2,0,1:T(4,128)(2,1)}), bf16[4,2048,128]{2,0,1:T(4,128)(2,1)}, u32[]{:S(2)}, u32[]{:S(2)}) async-start(bf16[4,2048,128]{2,0,1:T(4,128)(2,1)} %copy.137), calls=%async_computation.3 | async-start | bytes 4194304 | tf_op jit(solution)/shard_map/all_to_all | solution.py:137
  165.0 4.1 %copy.121 = f32[2,512,512]{1,2,0:T(8,128)} copy(f32[2,512,512]{2,0,1:T(2,128)} %bitcast.141) | data formatting | bytes 4194304 | tf_op jit(solution)/shard_map/while | solution.py:111
  169.1 43.7 %while.10 = (s32[]{:T(128)}, bf16[8,64,512]{2,1,0:T(8,128)(2,1)}, bf16[8,64,512]{2,1,0:T(8,128)(2,1)S(1)}, bf16[8,64,512]{2,1,0:T(8,128)(2,1)}, bf16[8,64,512]{2...) while((s32[]{:T(128)}, bf16[8,64,512]{2,1,0:T(8,128)(2,1)}, ...), condition=%wide.region_7.8_spmd, body=%wide.region_4.7_spmd.sunk | while | flops 70977536 | bytes 9517677 | solution.py:111
  170.8 2.1 add_add_fusion.2
  176.2 2.1 add_add_fusion.2
  181.7 2.1 add_add_fusion.2
  187.2 2.1 add_add_fusion.2
  192.6 2.1 add_add_fusion.2
  203.5 2.1 add_add_fusion.2
  209.0 2.1 add_add_fusion.2
  212.8 47.0 %all-gather.5.cloned.1.call-done = bf16[8,256,512]{2,1,0:T(8,128)(2,1)} async-done(((bf16[8,64,512]{2,1,0:T(8,128)(2,1)}), bf16[8,256,512]{2,1,0:T(8,128)(2,1)}) %all-gather.5.cloned.1.call-update) | async-done | bytes 2097168 | tf_op jit(solution)/shard_map/all_gather | solution.py:113
  259.8 4.3 %fusion.7 = bf16[8,512,256]{2,1,0:T(8,128)(2,1)} fusion(bf16[8,512,256]{2,1,0:T(8,128)(2,1)} %param.20, bf16[8,256,512]{2,1,0:T(8,128)(2,1)} %all-gather.5.cloned.1.call-done, bf16[256,256]{1,0:T(8,128)(2,1)S(1)} %copy-done), kind=kOutput, calls=%fused_computation.20 | convolution fusion | flops 540016640 | bytes 6422528 | tf_op jit(solution)/shard_map/sen,ec->snc/dot_general | solution.py:23
  264.1 2.1 fusion.44
  273.1 2.9 %copy.144 = bf16[64,128,128]{2,1,0:T(8,128)(2,1)} copy(bf16[64,128,128]{1,2,0:T(8,128)(2,1)S(1)} %add_convert_fusion) | data formatting | bytes 4194304
  (142 shorter events, 55.6 us)
Async XLA Ops:
  7.2 252.7 %copy-start = (bf16[256,256]{1,0:T(8,128)(2,1)S(1)}, bf16[256,256]{1,0:T(8,128)(2,1)}, u32[]{:S(2)}) copy-start(bf16[256,256]{1,0:T(8,128)(2,1)} %param.31) | copy-start | bytes 393220
  8.8 3.2 %copy-start.9 = (bf16[66,128]{1,0:T(8,128)(2,1)S(1)}, bf16[66,128]{1,0:T(8,128)(2,1)}, u32[]{:S(2)}) copy-start(bf16[66,128]{1,0:T(8,128)(2,1)} %param.25) | copy-start | bytes 50692
  13.8 2.0 copy-start.1
  15.7 0.8 copy-start.12
  16.6 21.2 %copy-start.3 = (bf16[64,128,128]{1,2,0:T(8,128)(2,1)}, bf16[64,128,128]{1,2,0:T(8,128)(2,1)S(1)}, u32[]{:S(2)}) copy-start(bf16[64,128,128]{1,2,0:T(8,128)(2,1)S(1)} %multiply_convert_fusion.2) | copy-start | bytes 6291460
  16.6 7.7 %copy-start.11 = (s32[512]{0:T(512)S(1)}, s32[512]{0:T(512)}, u32[]{:S(2)}) copy-start(s32[512]{0:T(512)} %param.22) | copy-start | bytes 6148
  16.6 7.9 %copy-start.6 = (bf16[128,128]{1,0:T(8,128)(2,1)S(1)}, bf16[128,128]{1,0:T(8,128)(2,1)}, u32[]{:S(2)}) copy-start(bf16[128,128]{1,0:T(8,128)(2,1)} %param.34) | copy-start | bytes 98308
  18.0 15.3 %all-to-all-start = ((f32[64,8,128]{2,0,1:T(8,128)}), f32[64,8,128]{2,0,1:T(8,128)S(1)}, u32[]{:S(2)}, u32[]{:S(2)}) async-start(f32[64,8,128]{2,0,1:T(8,128)} %copy.119), calls=%async_computation | async-start | bytes 524288 | tf_op jit(solution)/shard_map/all_to_all | solution.py:81
  24.5 0.8 copy-start.13
  29.5 7.5 %copy-start.7 = (bf16[128,128]{1,0:T(8,128)(2,1)S(1)}, bf16[128,128]{1,0:T(8,128)(2,1)}, u32[]{:S(2)}) copy-start(bf16[128,128]{1,0:T(8,128)(2,1)} %param.32) | copy-start | bytes 98308
  33.2 50.7 %all-to-all-start.2 = ((bf16[128,64,128]{2,1,0:T(8,128)(2,1)}), bf16[128,64,128]{2,1,0:T(8,128)(2,1)}, u32[]{:S(2)}, u32[]{:S(2)}) async-start(bf16[128,64,128]{2,1,0:T(8,128)(2,1)} %copy.133), calls=%async_computation.2 | async-start | bytes 4194304 | tf_op jit(solution)/shard_map/all_to_all | solution.py:130
  37.0 0.8 copy-start.14
  42.0 47.9 %copy-start.5 = (bf16[8,512,256]{2,1,0:T(8,128)(2,1)S(1)}, bf16[8,512,256]{2,1,0:T(8,128)(2,1)}, u32[]{:S(2)}) copy-start(bf16[8,512,256]{2,1,0:T(8,128)(2,1)} %param.20) | copy-start | bytes 6291460
  83.9 51.4 %all-to-all-start.1 = ((bf16[128,64,128]{2,1,0:T(8,128)(2,1)}), bf16[128,64,128]{2,1,0:T(8,128)(2,1)}, u32[]{:S(2)}, u32[]{:S(2)}) async-start(bf16[128,64,128]{2,1,0:T(8,128)(2,1)} %copy.126), calls=%async_computation.1 | async-start | bytes 4194304 | tf_op jit(solution)/shard_map/all_to_all | solution.py:129
  88.6 76.4 %all-gather.3.cloned.1.call-start = ((), (), s32[]{:S(2)}) async-start(), calls=%async_computation.4 | async-start | bytes 2359296 | tf_op jit(solution)/shard_map/all_gather | solution.py:90
  89.9 2.0 copy-start.10
  90.0 2.6 copy-start.15
  91.9 2.2 copy-start.16
  94.2 2.3 copy-start.17
  96.5 1.6 copy-start.18
  159.9 104.2 %all-to-all-start.3 = ((bf16[4,2048,128]{2,0,1:T(4,128)(2,1)}), bf16[4,2048,128]{2,0,1:T(4,128)(2,1)}, u32[]{:S(2)}, u32[]{:S(2)}) async-start(bf16[4,2048,128]{2,0,1:T(4,128)(2,1)} %copy.137), calls=%async_computation.3 | async-start | bytes 4194304 | tf_op jit(solution)/shard_map/all_to_all | solution.py:137
  165.0 94.9 %all-gather.5.cloned.1.call-start = ((), (), s32[]{:S(2)}) async-start(), calls=%async_computation.5 | async-start | bytes 2621440 | tf_op jit(solution)/shard_map/all_gather | solution.py:113
  267.8 0.8 copy-start.8
  268.6 2.2 copy-start.2
  268.6 2.9 %copy-start.4 = (bf16[64,128,128]{1,2,0:T(8,128)(2,1)S(1)}, bf16[64,128,128]{1,2,0:T(8,128)(2,1)}, u32[]{:S(2)}) copy-start(bf16[64,128,128]{1,2,0:T(8,128)(2,1)} %copy-done.3) | copy-start | bytes 6291460
  268.6 2.9 %copy-start.19 = (bf16[128,128]{1,0:T(8,128)(2,1)S(1)}, bf16[128,128]{1,0:T(8,128)(2,1)}, u32[]{:S(2)}) copy-start(bf16[128,128]{1,0:T(8,128)(2,1)} %param.36) | copy-start | bytes 98308
Sparse Core Ops, SparseCore 0:
  91.3 36.8 all-gather.2
  213.0 46.8 all-gather.4
where the time goes:
time: 285 us; the launch traced here: 283 us
  waiting for transfers between devices  122 us (43%)
  local copies, waits for them, and re-layouts  66.1 us (23%)
  matrix products  48.2 us (17%)
  starting transfers between devices  20.1 us (7%)
  between operations  14.5 us (5%)
  other arithmetic  12.1 us (4%)
    all_gather x1, waiting for transfers between devices, on_device(): lax.all_gather(attended, 'hc', axis=1, tiled=True)  47 us
    all_to_all x1, waiting for transfers between devices, on_device(): lax.all_to_all(right_side, ('dap', 'hc'), split_axis=0, concat_axis=1, ti...  41.9 us
    all_to_all x1, waiting for transfers between devices, on_device(): lax.all_to_all(left_side, ('dap', 'hc'), split_axis=0, concat_axis=1, til...  29.1 us
    dot_general x13, matrix products, project(): jnp.einsum(pattern, inputs, weight, preferred_element_type=jnp.float32)  21.9 us
    dot_general x8, matrix products, per_sequence(): jnp.einsum('hdi,hdj->hij', query_rows, keys_heads, preferred_element_type...  16.6 us
    dynamic_slice x24, local copies, waits for them, and re-layouts, on_device(): lax.map(per_sequence, (queries, keys_all, values_all, gates_all, key_bias))  13 us
    reshape x1, local copies, waits for them, and re-layouts, scramble(): return arranged.reshape(channels, dap_size * hc_size * row_count, col_count)  10.9 us
    unnamed x43, local copies, waits for them, and re-layouts  8.74 us
  transfers between devices with their start and end apart: 6, of which 4 were waited for; matrix products, arithmetic and copies ran while one was open for 36% of the time, Pallas kernels for 0%

commit v1 on v0

v1 whole, which is shorter than its diff:
```python
import jax
import jax.numpy as jnp
from jax import lax
from jax.experimental import pallas as pl
from jax.experimental.pallas import tpu as pltpu
from jax.sharding import PartitionSpec as P

HEAD_DIM = 32
REACH = 32


EPSILON = 1e-05
MASKED = 1000000000.0


def normalize(values, along):
    values = values.astype(jnp.float32)
    average = jnp.mean(values, axis=along, keepdims=True)
    centred = values - average
    variance = jnp.mean(centred * centred, axis=along, keepdims=True)
    return centred * lax.rsqrt(variance + EPSILON)


def project(inputs, weight, pattern):
    return jnp.einsum(pattern, inputs, weight, preferred_element_type=jnp.float32)


def attention_kernel(tile, query_ref, key_ref, value_ref, gate_ref, mask_ref, bias_ref, out_ref):
    width, residues = query_ref.shape[1:]
    keys = key_ref[0]
    masking = mask_ref[0]
    rows = lax.broadcasted_iota(jnp.int32, (width, tile), 0)
    for head in range(width // HEAD_DIM):
        own = slice(head * HEAD_DIM, (head + 1) * HEAD_DIM)
        for first in range(0, residues, tile):
            span = slice(first, first + tile)
            query = query_ref[0, :, span]
            query = jnp.where((rows >= own.start) & (rows < own.stop), query, jnp.zeros_like(query))
            scores = jnp.dot(keys, query, preferred_element_type=jnp.float32)
            scores = scores + bias_ref[head, :, span] + masking
            top = jnp.max(scores, axis=0, keepdims=True)
            weights = jnp.exp(scores - top)
            total = jnp.sum(weights, axis=0, keepdims=True)
            mixed = jnp.dot(
                value_ref[0, own, :], weights.astype(jnp.bfloat16), preferred_element_type=jnp.float32
            )
            gate = jax.nn.sigmoid(gate_ref[0, own, span].astype(jnp.float32))
            out_ref[0, own, span] = (mixed / total * gate).astype(jnp.bfloat16)


def attention(queries, keys, values, gates, masking, bias):
    count, width, residues = queries.shape
    tile = min(256, residues)
    wide = pl.BlockSpec((1, width, residues), lambda s: (s, 0, 0))
    return pl.pallas_call(
        lambda *refs: attention_kernel(tile, *refs),
        name="attention",
        grid=(count,),
        in_specs=[
            wide,
            pl.BlockSpec((1, residues, width), lambda s: (s, 0, 0)),
            wide,
            wide,
            pl.BlockSpec((1, residues, 1), lambda s: (s, 0, 0)),
            pl.BlockSpec(bias.shape, lambda s: (0, 0, 0)),
        ],
        out_specs=wide,
        out_shape=jax.ShapeDtypeStruct(queries.shape, jnp.bfloat16),
        cost_estimate=pl.CostEstimate(
            flops=32 * count * width * residues * residues,
            bytes_accessed=10 * count * width * residues + 4 * bias.size,
            transcendentals=count * bias.size,
        ),
    )(queries, keys, values, gates, masking, bias)


def triangle_kernel(left_ref, right_ref, out_ref):
    dap_size, hc_size, _, row_count, col_count = left_ref.shape

    def joined(ref):
        parts = [ref[:, h, 0].reshape(dap_size * row_count, col_count) for h in range(hc_size)]
        return jnp.concatenate(parts, axis=1)

    product = lax.dot_general(
        joined(left_ref), joined(right_ref), (((1,), (1,)), ((), ())), preferred_element_type=jnp.float32
    ).astype(jnp.bfloat16)
    for a in range(dap_size):
        for h in range(hc_size):
            out_ref[a, h, 0] = product[
                a * row_count : (a + 1) * row_count, h * col_count : (h + 1) * col_count
            ]


def triangle_product(left, right):
    dap_size, hc_size, channels, row_count, col_count = left.shape
    spec = pl.BlockSpec((dap_size, hc_size, 1, row_count, col_count), lambda c: (0, 0, c, 0, 0))
    return pl.pallas_call(
        triangle_kernel,
        name="triangle",
        grid=(channels,),
        in_specs=[spec, spec],
        out_specs=spec,
        out_shape=jax.ShapeDtypeStruct(left.shape, jnp.bfloat16),
        cost_estimate=pl.CostEstimate(
            flops=4 * left.size * dap_size * row_count, bytes_accessed=6 * left.size, transcendentals=0
        ),
    )(left, right)


def exchange(blocks):
    return lax.all_to_all(blocks, ("dap", "hc"), split_axis=0, concat_axis=0, tiled=True)


def on_device(
    alignment,
    align_mask,
    residue_mask,
    chain_index,
    pair_input,
    offset_table,
    bias_weight,
    query_weight,
    key_weight,
    value_weight,
    gate_weight,
    output_weight,
    left_gate_weight,
    left_weight,
    right_gate_weight,
    right_weight,
    update_gate_weight,
    update_out_weight,
):
    row_count = pair_input.shape[0]
    col_count = pair_input.shape[1]
    residues = residue_mask.shape[0]
    dap_size = lax.axis_size("dap")
    hc_size = lax.axis_size("hc")
    row_first = lax.axis_index("dap") * row_count
    col_first = lax.axis_index("hc") * col_count
    row_ids = row_first + jnp.arange(row_count, dtype=jnp.int32)
    col_ids = col_first + jnp.arange(col_count, dtype=jnp.int32)
    row_chain = lax.dynamic_slice_in_dim(chain_index, row_first, row_count, 0)
    col_chain = lax.dynamic_slice_in_dim(chain_index, col_first, col_count, 0)
    offsets = jnp.clip(row_ids[:, None] - col_ids[None, :] + REACH, 0, 2 * REACH)
    bin_index = jnp.where(row_chain[:, None] == col_chain[None, :], offsets, 2 * REACH + 1)
    slot_count = 128
    one_hot = (
        bin_index[:, :, None] == jnp.arange(slot_count, dtype=jnp.int32)[None, None, :]
    ).astype(jnp.bfloat16)
    padded_table = jnp.pad(offset_table, ((0, slot_count - offset_table.shape[0]), (0, 0)))
    pair_state = pair_input.astype(jnp.float32) + project(one_hot, padded_table, "ijb,bc->ijc")
    pair_norm = normalize(pair_state, 2).astype(jnp.bfloat16)
    head_bias = project(pair_norm, bias_weight, "ijc,ch->ihj")
    head_bias = lax.all_to_all(head_bias, "hc", split_axis=1, concat_axis=2, tiled=True)
    align_norm = normalize(alignment, 2).astype(jnp.bfloat16)
    scaling = HEAD_DIM ** (-0.5)
    queries = (project(align_norm, query_weight, "snc,ce->sen") * scaling).astype(jnp.bfloat16)
    keys_all = project(align_norm, key_weight, "snc,ce->sne").astype(jnp.bfloat16)
    values_all = project(align_norm, value_weight, "snc,ce->sen").astype(jnp.bfloat16)
    gates_all = project(align_norm, gate_weight, "snc,ce->sen").astype(jnp.bfloat16)
    key_bias = MASKED * ((align_mask * residue_mask[None, :]).astype(jnp.float32) - 1.0)
    bias_rows = lax.all_gather(head_bias, "dap", axis=0, tiled=True)
    residue_rows = lax.dynamic_slice_in_dim(residue_mask, row_first, row_count, 0)
    residue_cols = lax.dynamic_slice_in_dim(residue_mask, col_first, col_count, 0)
    pair_mask = (residue_rows[:, None] * residue_cols[None, :]).astype(jnp.float32)
    update_gate = jax.nn.sigmoid(project(pair_norm, update_gate_weight, "ijc,ce->ije"))
    left_side = jax.nn.sigmoid(project(pair_norm, left_gate_weight, "ijc,ce->eij")) * project(
        pair_norm, left_weight, "ijc,ce->eij"
    )
    left_side = (left_side * pair_mask[None, :, :]).astype(jnp.bfloat16)
    right_side = jax.nn.sigmoid(project(pair_norm, right_gate_weight, "ijc,ce->eij")) * project(
        pair_norm, right_weight, "ijc,ce->eij"
    )
    right_side = (right_side * pair_mask[None, :, :]).astype(jnp.bfloat16)
    own_channels = left_side.shape[0] // (dap_size * hc_size)
    shares = (dap_size, hc_size, own_channels, row_count, col_count)
    right_all = exchange(right_side).reshape(shares)
    left_side, bias_rows = lax.optimization_barrier((left_side, bias_rows))
    left_all = exchange(left_side).reshape(shares)
    bias_heads = jnp.transpose(bias_rows, (1, 2, 0))
    attended = attention(queries, keys_all, values_all, gates_all, key_bias[:, :, None], bias_heads)
    triangle = triangle_product(left_all, right_all)
    triangle, attended = lax.optimization_barrier((triangle, attended))
    triangle_local = exchange(triangle.reshape(left_side.shape))
    merged = project(
        lax.all_gather(attended, "hc", axis=1, tiled=True), output_weight, "sen,ec->snc"
    )
    alignment_out = (alignment.astype(jnp.float32) + merged).astype(jnp.bfloat16)
    triangle_norm = normalize(triangle_local, 0).astype(jnp.bfloat16)
    update = project(triangle_norm, update_out_weight, "eij,ec->ijc") * update_gate
    pair_out = (pair_state + update).astype(jnp.bfloat16)
    return (alignment_out, pair_out)


def solution(mesh):
    placed = (
        P("dap", None, None),
        P("dap", None),
        P(),
        P(),
        P("dap", "hc", None),
        P(),
        P(),
        P(None, "hc"),
        P(None, "hc"),
        P(None, "hc"),
        P(None, "hc"),
        P(),
        P(),
        P(),
        P(),
        P(),
        P(),
        P(),
    )
    return jax.shard_map(
        on_device,
        mesh=mesh,
        in_specs=placed,
        out_specs=(P("dap", None, None), P("dap", "hc", None)),
        check_vma=False,
    )
```

time: 285 us -> 254 us (0.89)
  local copies, waits for them, and re-layouts: 66.1 us -> 26.3 us
  Pallas kernels: 0 us -> 20.8 us
  matrix products: 48.2 us -> 27.8 us
  waiting for transfers between devices: 122 us -> 131 us
    all_to_all x3, waiting for transfers between devices: 71 us -> 10.2 us  [exchange(): lax.all_to_all(blocks, ('dap', 'hc'), split_axis=0, concat_axis=0, tiled=...]
    all_gather x1, waiting for transfers between devices: 0.02 us -> 34.8 us  [on_device(): bias_rows = lax.all_gather(head_bias, 'dap', axis=0, tiled=True)]
    all_gather x1, waiting for transfers between devices: 47 us -> 81.3 us  [on_device(): lax.all_gather(attended, 'hc', axis=1, tiled=True)]
    dot_general x17 -> x0, matrix products: 26.4 us -> none  [the longest x8 16.6 us: per_sequence(): jnp.einsum('hdi,hdj->hij', query_rows, keys_heads, preferred_element_type...]
    pallas_call x0 -> x2, Pallas kernels: none -> 20.8 us  [the longest x1 15.7 us: attention(): pl.pallas_call(lambda *refs: attention_kernel(tile, *refs), name='attenti...]
    reshape x5 -> x0, local copies, waits for them, and re-layouts: 18.4 us -> none  [the longest x1 10.9 us: scramble(): return arranged.reshape(channels, dap_size * hc_size * row_count, col_count)]
    dynamic_slice x24 -> x0, local copies, waits for them, and re-layouts: 13 us -> none  [on_device(): lax.map(per_sequence, (queries, keys_all, values_all, gates_all, key_bias))]
    optimization_barrier x0 -> x2, local copies, waits for them, and re-layouts: none -> 8.42 us  [on_device(): left_side, bias_rows = lax.optimization_barrier((left_side, bias_rows))]
  transfers between devices with their start and end apart: 6 -> 6, of which waited for: 4 -> 5; matrix products, arithmetic and copies ran while one was open for 36% -> 16% of each run, Pallas kernels for 0% -> 6%
where the time goes in v1:
time: 254 us; the launch traced here: 253 us
  waiting for transfers between devices  131 us (52%)
  matrix products  27.8 us (11%)
  local copies, waits for them, and re-layouts  26.3 us (10%)
  Pallas kernels  20.8 us (8%)
  starting transfers between devices  20.1 us (8%)
  between operations  14.4 us (6%)
  other arithmetic  13.1 us (5%)
    all_gather x1, waiting for transfers between devices, on_device(): lax.all_gather(attended, 'hc', axis=1, tiled=True)  81.3 us
    all_gather x1, waiting for transfers between devices, on_device(): bias_rows = lax.all_gather(head_bias, 'dap', axis=0, tiled=True)  34.8 us
    dot_general x13, matrix products, project(): jnp.einsum(pattern, inputs, weight, preferred_element_type=jnp.float32)  27.8 us
    pallas_call x1, Pallas kernels, attention(): pl.pallas_call(lambda *refs: attention_kernel(tile, *refs), name='attenti...  15.7 us
    all_to_all x3, starting transfers between devices, exchange(): lax.all_to_all(blocks, ('dap', 'hc'), split_axis=0, concat_axis=0, tiled=...  13.7 us
    all_to_all x3, waiting for transfers between devices, exchange(): lax.all_to_all(blocks, ('dap', 'hc'), split_axis=0, concat_axis=0, tiled=...  10.2 us
    optimization_barrier x2, local copies, waits for them, and re-layouts, on_device(): left_side, bias_rows = lax.optimization_barrier((left_side, bias_rows))  8.42 us
    unnamed x41, local copies, waits for them, and re-layouts  8.3 us
  transfers between devices with their start and end apart: 6, of which 5 were waited for; matrix products, arithmetic and copies ran while one was open for 16% of the time, Pallas kernels for 6%

profile of v1, /device:TPU:0, one launch (start us, length us, event | category | flops | bytes accessed | tf_op | source)
XLA Modules:
  0.0 253.1 jit_solution(11433802054107115419)
XLA Ops:
  8.8 3.2 %copy.84 = bf16[64,128,128]{1,2,0:T(8,128)(2,1)S(1)} copy(bf16[64,128,128]{2,1,0:T(8,128)(2,1)} %param.22) | data formatting | bytes 4194304 | tf_op args[4]
  12.2 1.6 fusion.40
  16.9 6.3 %all-to-all-start = ((f32[64,8,128]{2,0,1:T(8,128)}), f32[64,8,128]{2,0,1:T(8,128)S(1)}, u32[]{:S(2)}, u32[]{:S(2)}) async-start(f32[64,8,128]{2,0,1:T(8,128)} %copy.91), calls=%async_computation | async-start | bytes 524288 | tf_op jit(solution)/shard_map/all_to_all | solution.py:155
  24.2 1.6 fusion.14
  25.8 2.7 %copy.98 = bf16[128,64,128]{2,1,0:T(8,128)(2,1)} copy(bf16[128,64,128]{2,0,1:T(8,128)(2,1)S(1)} %fusion.14) | data formatting | bytes 4194304 | tf_op jit(solution)/shard_map/convert_element_type | solution.py:175
  28.5 3.7 %all-to-all-done = f32[64,8,128]{2,0,1:T(8,128)S(1)} async-done(((f32[64,8,128]{2,0,1:T(8,128)}), f32[64,8,128]{2,0,1:T(8,128)S(1)}, u32[]{:S(2)}, u32[]{:S(2)}) %all-to-all-start) | async-done | bytes 262176 | tf_op jit(solution)/shard_map/all_to_all | solution.py:155
  32.2 3.8 %all-to-all-start.2 = ((bf16[128,64,128]{2,1,0:T(8,128)(2,1)}), bf16[128,64,128]{2,1,0:T(8,128)(2,1)}, u32[]{:S(2)}, u32[]{:S(2)}) async-start(bf16[128,64,128]{2,1,0:T(8,128)(2,1)} %copy.98), calls=%async_computation.2 | async-start | bytes 4194304 | tf_op jit(solution)/shard_map/all_to_all | solution.py:111
  37.9 2.9 %fusion.13 = bf16[128,64,128]{2,0,1:T(8,128)(2,1)} fusion(f32[64,128]{1,0:T(8,128)S(1)} %multiply_convert_fusion.3, bf16[64,128,128]{1,2,0:T(8,128)(2,1)S(1)} %multiply_convert_fusion.2, f32[64,128,128]{1,2,0:T(8,128)S(1)} %fusion.34, bf16[128,128]{1,0:T(8,128)(2,1)S(1)} %copy-done.13), kind=kOutput, calls=%fused_computation.25 | convolution fusion | flops 274726912 | bytes 8454144 | tf_op jit(solution)/shard_map/ijc,ce->eij/dot_general | solution.py:25
  40.8 34.8 %all-gather.3.cloned.1.call-done = f32[512,2,512]{2,1,0:T(2,128)} async-done(((f32[64,2,512]{2,1,0:T(2,128)}), f32[512,2,512]{2,1,0:T(2,128)}) %all-gather.3.cloned.1.call-update) | async-done | bytes 2097168 | tf_op jit(solution)/shard_map/all_gather | solution.py:163
  75.5 4.3 %copy.93 = bf16[128,64,128]{2,1,0:T(8,128)(2,1)} copy(bf16[128,64,128]{2,0,1:T(8,128)(2,1)} %fusion.13) | data formatting | bytes 4194304 | tf_op jit(solution)/shard_map/optimization_barrier | solution.py:179
  79.8 3.0 %all-to-all-done.2 = bf16[128,64,128]{2,1,0:T(8,128)(2,1)} async-done(((bf16[128,64,128]{2,1,0:T(8,128)(2,1)}), bf16[128,64,128]{2,1,0:T(8,128)(2,1)}, u32[]{:S(2)}, u32[]{:S(2)}) %all-to-all-start.2) | async-done | bytes 2097184 | tf_op jit(solution)/shard_map/all_to_all | solution.py:111
  82.8 4.9 %all-to-all-start.1 = ((bf16[128,64,128]{2,1,0:T(8,128)(2,1)}), bf16[128,64,128]{2,1,0:T(8,128)(2,1)}, u32[]{:S(2)}, u32[]{:S(2)}) async-start(bf16[128,64,128]{2,1,0:T(8,128)(2,1)} %copy.93), calls=%async_computation.1 | async-start | bytes 4194304 | tf_op jit(solution)/shard_map/all_to_all | solution.py:111
  87.7 2.4 convert_reduce_fusion
  90.1 2.5 %fusion.4 = f32[8,512]{1,0:T(8,128)S(1)} fusion(bf16[8,512,256]{2,1,0:T(8,128)(2,1)} %param.18, f32[8,512]{1,0:T(8,128)S(1)} %broadcast_multiply_fusion.2), kind=kLoop, calls=%fused_computation.9 | loop fusion | flops 4190208 | bytes 2129920 | tf_op jit(solution)/shard_map/reduce_sum | solution.py:20
  92.7 1.6 convolution_convert_fusion.2
  95.7 2.0 copy.101.refs_4_
  97.7 3.7 %fusion.16.refs_2_ = bf16[8,64,512]{2,1,0:T(8,128)(2,1)} fusion(bf16[8,512,256]{2,1,0:T(8,128)(2,1)} %param.18, f32[8,512]{1,0:T(8,128)S(1)} %add_rsqrt_fusion.2, f32[8,512]{1,0:T(8,128)S(1)} %broadcast_multiply_fusion.2, bf16[256,64]{0,1:T(8,128)(2,1)S(1)} %copy-done.15), kind=kOutput, calls=%fused_computation.32 | convolution fusion | flops 138674176 | bytes 2686976 | tf_op jit(solution)/shard_map/snc,ce->sen/dot_general | solution.py:25
  101.4 3.5 %fusion.17.refs_3_ = bf16[8,64,512]{2,1,0:T(8,128)(2,1)} fusion(bf16[8,512,256]{2,1,0:T(8,128)(2,1)} %param.18, f32[8,512]{1,0:T(8,128)S(1)} %add_rsqrt_fusion.2, f32[8,512]{1,0:T(8,128)S(1)} %broadcast_multiply_fusion.2, bf16[256,64]{0,1:T(8,128)(2,1)S(1)} %copy-done.16), kind=kOutput, calls=%fused_computation.33 | convolution fusion | flops 138674176 | bytes 2686976 | tf_op jit(solution)/shard_map/snc,ce->sen/dot_general | solution.py:25
  104.9 2.3 fusion.18.refs_0_
  107.2 4.1 %copy.99 = f32[512,2,512]{0,2,1:T(8,128)} copy(f32[512,2,512]{2,1,0:T(2,128)} %all-gather.3.cloned.1.call-done) | data formatting | bytes 4194304 | tf_op jit(solution)/shard_map/optimization_barrier | solution.py:179
  111.3 15.7 %attention.1 = bf16[8,64,512]{2,1,0:T(8,128)(2,1)} custom-call(bf16[8,64,512]{2,1,0:T(8,128)(2,1)} %fusion.18.refs_0_, bf16[8,512,64]{2,1,0:T(8,128)(2,1)} %copy.100.refs_1_, bf16[8,64,512]{2,1,0:T(8,128)(2,1)} %fusion.16.refs_2_, bf16[8,64,512]{2,1,0:T(8,128)(2,1)} %fusion.17.refs_3_, f32[8,512,1]{2,1,0:T(8,128)} %copy.101.refs_4_, f32[2,512,512]{2,1,0:T(8,128)} %bitcast.70), custom_call_target="tpu_custom_call" | custom-call | flops 4294967296 | bytes 4718592 | tf_op jit(solution)/shard_map/attention/pallas_call | solution.py:55
  127.1 7.1 %all-to-all-done.1 = bf16[128,64,128]{2,1,0:T(8,128)(2,1)} async-done(((bf16[128,64,128]{2,1,0:T(8,128)(2,1)}), bf16[128,64,128]{2,1,0:T(8,128)(2,1)}, u32[]{:S(2)}, u32[]{:S(2)}) %all-to-all-start.1) | async-done | bytes 2097184 | tf_op jit(solution)/shard_map/all_to_all | solution.py:111
  134.2 5.0 %triangle.1 = bf16[8,4,4,64,128]{4,3,2,1,0:T(8,128)(2,1)} custom-call(bf16[8,4,4,64,128]{4,3,2,1,0:T(8,128)(2,1)} %bitcast.8.left_ref, bf16[8,4,4,64,128]{4,3,2,1,0:T(8,128)(2,1)} %bitcast.12.right_ref), custom_call_target="tpu_custom_call" | custom-call | flops 2147483648 | bytes 6291456 | tf_op jit(solution)/shard_map/triangle/pallas_call | solution.py:97
  139.2 5.0 %all-to-all-start.3 = ((bf16[128,64,128]{2,1,0:T(8,128)(2,1)}), bf16[128,64,128]{2,1,0:T(8,128)(2,1)}, u32[]{:S(2)}, u32[]{:S(2)}) async-start(bf16[128,64,128]{2,1,0:T(8,128)(2,1)} %bitcast.69), calls=%async_computation.3 | async-start | bytes 4194304 | tf_op jit(solution)/shard_map/all_to_all | solution.py:111
  145.0 81.3 %all-gather.5.cloned.1.call-done = bf16[8,256,512]{2,1,0:T(8,128)(2,1)} async-done(((bf16[8,64,512]{2,1,0:T(8,128)(2,1)}), bf16[8,256,512]{2,1,0:T(8,128)(2,1)}) %all-gather.5.cloned.1.call-update) | async-done | bytes 2097168 | tf_op jit(solution)/shard_map/all_gather | solution.py:187
  226.3 4.3 %fusion.8 = bf16[8,512,256]{2,1,0:T(8,128)(2,1)} fusion(bf16[8,512,256]{2,1,0:T(8,128)(2,1)} %param.18, bf16[8,256,512]{2,1,0:T(8,128)(2,1)} %all-gather.5.cloned.1.call-done, bf16[256,256]{1,0:T(8,128)(2,1)S(1)} %copy-done), kind=kOutput, calls=%fused_computation.13 | convolution fusion | flops 540016640 | bytes 6422528 | tf_op jit(solution)/shard_map/sen,ec->snc/dot_general | solution.py:25
  230.7 2.0 convert_reduce_fusion.1
  232.6 2.2 fusion.6
  234.8 2.3 fusion.7
  237.1 1.6 fusion.10
  239.3 2.9 %add_convert_fusion = bf16[64,128,128]{1,2,0:T(8,128)(2,1)} fusion(f32[64,128,128]{1,2,0:T(8,128)S(1)} %copy-done.2, f32[64,128,128]{1,2,0:T(8,128)S(1)} %fusion.10, bf16[64,128,128]{1,2,0:T(8,128)(2,1)S(1)} %multiply_convert_fusion.2, bf16[128,128]{1,0:T(8,128)(2,1)S(1)} %copy-done.18), kind=kOutput, calls=%fused_computation.16 | convolution fusion | flops 274726912 | bytes 12615680 | tf_op jit(solution)/shard_map/ijc,ce->ije/dot_general | solution.py:25
  242.2 4.1 %copy.106 = bf16[64,128,128]{2,1,0:T(8,128)(2,1)} copy(bf16[64,128,128]{1,2,0:T(8,128)(2,1)} %add_convert_fusion) | data formatting | bytes 4194304
  (68 shorter events, 10.4 us)
Async XLA Ops:
  7.2 219.2 %copy-start = (bf16[256,256]{1,0:T(8,128)(2,1)S(1)}, bf16[256,256]{1,0:T(8,128)(2,1)}, u32[]{:S(2)}) copy-start(bf16[256,256]{1,0:T(8,128)(2,1)} %param.29) | copy-start | bytes 393220
  7.2 4.8 %copy-start.8 = (bf16[66,128]{1,0:T(8,128)(2,1)S(1)}, bf16[66,128]{1,0:T(8,128)(2,1)}, u32[]{:S(2)}) copy-start(bf16[66,128]{1,0:T(8,128)(2,1)} %param.23) | copy-start | bytes 50692
  13.8 2.0 copy-start.1
  14.6 1.2 copy-start.11
  14.6 8.6 %copy-start.10 = (s32[512]{0:T(512)S(1)}, s32[512]{0:T(512)}, u32[]{:S(2)}) copy-start(s32[512]{0:T(512)} %param.20) | copy-start | bytes 6148
  14.6 8.8 %copy-start.5 = (bf16[128,128]{1,0:T(8,128)(2,1)S(1)}, bf16[128,128]{1,0:T(8,128)(2,1)}, u32[]{:S(2)}) copy-start(bf16[128,128]{1,0:T(8,128)(2,1)} %param.32) | copy-start | bytes 98308
  16.1 8.1 %copy-start.12 = (bf16[128,128]{1,0:T(8,128)(2,1)S(1)}, bf16[128,128]{1,0:T(8,128)(2,1)}, u32[]{:S(2)}) copy-start(bf16[128,128]{1,0:T(8,128)(2,1)} %param.33) | copy-start | bytes 98308
  16.9 15.3 %all-to-all-start = ((f32[64,8,128]{2,0,1:T(8,128)}), f32[64,8,128]{2,0,1:T(8,128)S(1)}, u32[]{:S(2)}, u32[]{:S(2)}) async-start(f32[64,8,128]{2,0,1:T(8,128)} %copy.91), calls=%async_computation | async-start | bytes 524288 | tf_op jit(solution)/shard_map/all_to_all | solution.py:155
  25.8 11.3 %copy-start.6 = (bf16[128,128]{1,0:T(8,128)(2,1)S(1)}, bf16[128,128]{1,0:T(8,128)(2,1)}, u32[]{:S(2)}) copy-start(bf16[128,128]{1,0:T(8,128)(2,1)} %param.30) | copy-start | bytes 98308
  32.2 50.7 %all-to-all-start.2 = ((bf16[128,64,128]{2,1,0:T(8,128)(2,1)}), bf16[128,64,128]{2,1,0:T(8,128)(2,1)}, u32[]{:S(2)}, u32[]{:S(2)}) async-start(bf16[128,64,128]{2,1,0:T(8,128)(2,1)} %copy.98), calls=%async_computation.2 | async-start | bytes 4194304 | tf_op jit(solution)/shard_map/all_to_all | solution.py:111
  36.0 1.9 copy-start.13
  36.0 39.5 %all-gather.3.cloned.1.call-start = ((), (), s32[]{:S(2)}) async-start(), calls=%async_computation.4 | async-start | bytes 2359296 | tf_op jit(solution)/shard_map/all_gather | solution.py:163
  79.8 12.9 %copy-start.14 = (bf16[256,64]{0,1:T(8,128)(2,1)S(1)}, bf16[256,64]{0,1:T(8,128)(2,1)}, u32[]{:S(2)}) copy-start(bf16[256,64]{0,1:T(8,128)(2,1)} %param.26) | copy-start | bytes 98308
  82.8 51.4 %all-to-all-start.1 = ((bf16[128,64,128]{2,1,0:T(8,128)(2,1)}), bf16[128,64,128]{2,1,0:T(8,128)(2,1)}, u32[]{:S(2)}, u32[]{:S(2)}) async-start(bf16[128,64,128]{2,1,0:T(8,128)(2,1)} %copy.93), calls=%async_computation.1 | async-start | bytes 4194304 | tf_op jit(solution)/shard_map/all_to_all | solution.py:111
  87.7 5.0 %copy-start.3 = (bf16[8,512,256]{2,1,0:T(8,128)(2,1)S(1)}, bf16[8,512,256]{2,1,0:T(8,128)(2,1)}, u32[]{:S(2)}) copy-start(bf16[8,512,256]{2,1,0:T(8,128)(2,1)} %param.18) | copy-start | bytes 6291460
  90.1 5.6 %copy-start.9 = (s32[8,512]{1,0:T(8,128)S(1)}, s32[8,512]{1,0:T(8,128)}, u32[]{:S(2)}) copy-start(s32[8,512]{1,0:T(8,128)} %param.19) | copy-start | bytes 49156
  92.7 5.0 %copy-start.15 = (bf16[256,64]{0,1:T(8,128)(2,1)S(1)}, bf16[256,64]{0,1:T(8,128)(2,1)}, u32[]{:S(2)}) copy-start(bf16[256,64]{0,1:T(8,128)(2,1)} %param.27) | copy-start | bytes 98308
  94.3 7.0 %copy-start.16 = (bf16[256,64]{0,1:T(8,128)(2,1)S(1)}, bf16[256,64]{0,1:T(8,128)(2,1)}, u32[]{:S(2)}) copy-start(bf16[256,64]{0,1:T(8,128)(2,1)} %param.28) | copy-start | bytes 98308
  97.7 7.2 %copy-start.4 = (bf16[8,512,256]{2,1,0:T(8,128)(2,1)S(1)}, bf16[8,512,256]{2,1,0:T(8,128)(2,1)}, u32[]{:S(2)}) copy-start(bf16[8,512,256]{2,1,0:T(8,128)(2,1)} %param.18) | copy-start | bytes 6291460
  97.7 7.2 %copy-start.17 = (bf16[256,64]{0,1:T(8,128)(2,1)S(1)}, bf16[256,64]{0,1:T(8,128)(2,1)}, u32[]{:S(2)}) copy-start(bf16[256,64]{0,1:T(8,128)(2,1)} %param.25) | copy-start | bytes 98308
  139.2 91.4 %all-to-all-start.3 = ((bf16[128,64,128]{2,1,0:T(8,128)(2,1)}), bf16[128,64,128]{2,1,0:T(8,128)(2,1)}, u32[]{:S(2)}, u32[]{:S(2)}) async-start(bf16[128,64,128]{2,1,0:T(8,128)(2,1)} %bitcast.69), calls=%async_computation.3 | async-start | bytes 4194304 | tf_op jit(solution)/shard_map/all_to_all | solution.py:111
  144.3 82.1 %all-gather.5.cloned.1.call-start = ((), (), s32[]{:S(2)}) async-start(), calls=%async_computation.5 | async-start | bytes 2621440 | tf_op jit(solution)/shard_map/all_gather | solution.py:187
  230.6 6.4 %copy-start.7 = (bf16[128,128]{1,0:T(8,128)(2,1)S(1)}, bf16[128,128]{1,0:T(8,128)(2,1)}, u32[]{:S(2)}) copy-start(bf16[128,128]{1,0:T(8,128)(2,1)} %param.35) | copy-start | bytes 98308
  237.1 2.2 copy-start.2
  237.1 2.2 copy-start.18
Sparse Core Ops, SparseCore 0:
  38.7 36.7 all-gather.2
  146.6 79.6 all-gather.4

commit v2 on v1

--- a/solution.py
+++ b/solution.py
@@ -109,6 +109,28 @@
 
 def exchange(blocks):
     return lax.all_to_all(blocks, ("dap", "hc"), split_axis=0, concat_axis=0, tiled=True)
+
+
+def line_steps(early, step):
+    size = lax.axis_size("hc")
+    up = [(i, i + 1) for i in range(step - 1, size - 1)]
+    down = [(i + 1, i) for i in range(size - step)]
+    return lax.ppermute(early[0], "hc", up), lax.ppermute(early[1], "hc", down)
+
+
+def line_gather(block, first, weight):
+    size = lax.axis_size("hc")
+    here = lax.axis_index("hc")
+    width = block.shape[1]
+    passed = [(block, block), first]
+    for step in range(2, size):
+        passed.append(line_steps(passed[-1], step))
+    pieces = [block] + [passed[step][0] + passed[size - step][1] for step in range(1, size)]
+    rows = [
+        lax.dynamic_slice_in_dim(weight, lax.rem(here - step + size, size) * width, width, 0)
+        for step in range(size)
+    ]
+    return jnp.concatenate(pieces, axis=1), jnp.concatenate(rows, axis=0)
 
 
 def on_device(
@@ -175,17 +197,18 @@
     right_side = (right_side * pair_mask[None, :, :]).astype(jnp.bfloat16)
     own_channels = left_side.shape[0] // (dap_size * hc_size)
     shares = (dap_size, hc_size, own_channels, row_count, col_count)
+    left_all = exchange(left_side).reshape(shares)
+    right_side, bias_rows, left_all = lax.optimization_barrier((right_side, bias_rows, left_all))
     right_all = exchange(right_side).reshape(shares)
-    left_side, bias_rows = lax.optimization_barrier((left_side, bias_rows))
-    left_all = exchange(left_side).reshape(shares)
     bias_heads = jnp.transpose(bias_rows, (1, 2, 0))
     attended = attention(queries, keys_all, values_all, gates_all, key_bias[:, :, None], bias_heads)
+    first = line_steps((attended, attended), 1)
+    right_all, first = lax.optimization_barrier((right_all, first))
     triangle = triangle_product(left_all, right_all)
     triangle, attended = lax.optimization_barrier((triangle, attended))
     triangle_local = exchange(triangle.reshape(left_side.shape))
-    merged = project(
-        lax.all_gather(attended, "hc", axis=1, tiled=True), output_weight, "sen,ec->snc"
-    )
+    pieces, weight = line_gather(attended, first, output_weight)
+    merged = project(pieces, weight, "sen,ec->snc")
     alignment_out = (alignment.astype(jnp.float32) + merged).astype(jnp.bfloat16)
     triangle_norm = normalize(triangle_local, 0).astype(jnp.bfloat16)
     update = project(triangle_norm, update_out_weight, "eij,ec->ijc") * update_gate

time: 254 us -> 262 us (1.031)
  starting transfers between devices: 20.1 us -> 30.6 us
  waiting for transfers between devices: 131 us -> 127 us
  other arithmetic: 13.1 us -> 17 us
    all_gather x1 -> x0, waiting for transfers between devices: 81.3 us -> none  [on_device(): lax.all_gather(attended, 'hc', axis=1, tiled=True)]
    ppermute x0 -> x6, waiting for transfers between devices: none -> 80.7 us  [the longest x3 71 us: line_steps(): lax.ppermute(early[1], 'hc', down)]
    all_gather x1, waiting for transfers between devices: 34.8 us -> 0.01 us  [on_device(): bias_rows = lax.all_gather(head_bias, 'dap', axis=0, tiled=True)]
    all_to_all x3, waiting for transfers between devices: 10.2 us -> 42.1 us  [exchange(): lax.all_to_all(blocks, ('dap', 'hc'), split_axis=0, concat_axis=0, tiled=...]
    ppermute x0 -> x6, starting transfers between devices: none -> 11 us  [the longest x3 7.11 us: line_steps(): lax.ppermute(early[0], 'hc', up)]
    add x0 -> x3, other arithmetic: none -> 3.85 us  [line_gather(): passed[step][0] + passed[size - step][1]]
    unnamed x41 -> x47, local copies, waits for them, and re-layouts: 8.3 us -> 8.29 us
  transfers between devices with their start and end apart: 6 -> 11, of which waited for: 5 -> 6; matrix products, arithmetic and copies ran while one was open for 16% -> 15% of each run, Pallas kernels for 6% -> 6%
where the time goes in v2:
time: 262 us; the launch traced here: 261 us
  waiting for transfers between devices  127 us (48%)
  starting transfers between devices  30.6 us (12%)
  local copies, waits for them, and re-layouts  26.3 us (10%)
  matrix products  25.6 us (10%)
  Pallas kernels  20.8 us (8%)
  other arithmetic  17 us (6%)
  between operations  14.5 us (6%)
    ppermute x3, waiting for transfers between devices, line_steps(): lax.ppermute(early[1], 'hc', down)  71 us
    all_to_all x3, waiting for transfers between devices, exchange(): lax.all_to_all(blocks, ('dap', 'hc'), split_axis=0, concat_axis=0, tiled=...  42.1 us
    dot_general x13, matrix products, project(): jnp.einsum(pattern, inputs, weight, preferred_element_type=jnp.float32)  25.6 us
    pallas_call x1, Pallas kernels, attention(): pl.pallas_call(lambda *refs: attention_kernel(tile, *refs), name='attenti...  15.7 us
    all_to_all x3, starting transfers between devices, exchange(): lax.all_to_all(blocks, ('dap', 'hc'), split_axis=0, concat_axis=0, tiled=...  13.3 us
    ppermute x3, waiting for transfers between devices, line_steps(): lax.ppermute(early[0], 'hc', up)  9.71 us
    optimization_barrier x2, local copies, waits for them, and re-layouts, on_device(): lax.optimization_barrier((right_side, bias_rows, left_all))  8.45 us
    unnamed x47, local copies, waits for them, and re-layouts  8.29 us
  transfers between devices with their start and end apart: 11, of which 6 were waited for; matrix products, arithmetic and copies ran while one was open for 15% of the time, Pallas kernels for 6%

profile of v2, /device:TPU:0, one launch (start us, length us, event | category | flops | bytes accessed | tf_op | source)
XLA Modules:
  0.0 261.2 jit_solution(3593146316102876229)
XLA Ops:
  8.7 3.2 %copy.87 = bf16[64,128,128]{1,2,0:T(8,128)(2,1)S(1)} copy(bf16[64,128,128]{2,1,0:T(8,128)(2,1)} %param.22) | data formatting | bytes 4194304 | tf_op args[4]
  16.8 6.3 %all-to-all-start = ((f32[64,8,128]{2,0,1:T(8,128)}), f32[64,8,128]{2,0,1:T(8,128)S(1)}, u32[]{:S(2)}, u32[]{:S(2)}) async-start(f32[64,8,128]{2,0,1:T(8,128)} %copy.94), calls=%async_computation | async-start | bytes 524288 | tf_op jit(solution)/shard_map/all_to_all | solution.py:177
  25.7 2.7 %copy.100 = bf16[128,64,128]{2,1,0:T(8,128)(2,1)} copy(bf16[128,64,128]{2,0,1:T(8,128)(2,1)S(1)} %fusion.21) | data formatting | bytes 4194304 | tf_op jit(solution)/shard_map/convert_element_type | solution.py:193
  28.4 3.7 %all-to-all-done = f32[64,8,128]{2,0,1:T(8,128)S(1)} async-done(((f32[64,8,128]{2,0,1:T(8,128)}), f32[64,8,128]{2,0,1:T(8,128)S(1)}, u32[]{:S(2)}, u32[]{:S(2)}) %all-to-all-start) | async-done | bytes 262176 | tf_op jit(solution)/shard_map/all_to_all | solution.py:177
  32.1 3.8 %all-to-all-start.1 = ((bf16[128,64,128]{2,1,0:T(8,128)(2,1)}), bf16[128,64,128]{2,1,0:T(8,128)(2,1)}, u32[]{:S(2)}, u32[]{:S(2)}) async-start(bf16[128,64,128]{2,1,0:T(8,128)(2,1)} %copy.100), calls=%async_computation.1 | async-start | bytes 4194304 | tf_op jit(solution)/shard_map/all_to_all | solution.py:111
  37.8 2.9 %fusion.20 = bf16[128,64,128]{2,0,1:T(8,128)(2,1)} fusion(f32[64,128]{1,0:T(8,128)S(1)} %multiply_convert_fusion.3, bf16[64,128,128]{1,2,0:T(8,128)(2,1)S(1)} %multiply_convert_fusion.2, f32[64,128,128]{1,2,0:T(8,128)S(1)} %fusion.46, bf16[128,128]{1,0:T(8,128)(2,1)S(1)} %copy-done.16), kind=kOutput, calls=%fused_computation.32 | convolution fusion | flops 274726912 | bytes 8454144 | tf_op jit(solution)/shard_map/ijc,ce->eij/dot_general | solution.py:25
  40.7 42.1 %all-to-all-done.1 = bf16[128,64,128]{2,1,0:T(8,128)(2,1)} async-done(((bf16[128,64,128]{2,1,0:T(8,128)(2,1)}), bf16[128,64,128]{2,1,0:T(8,128)(2,1)}, u32[]{:S(2)}, u32[]{:S(2)}) %all-to-all-start.1) | async-done | bytes 2097184 | tf_op jit(solution)/shard_map/all_to_all | solution.py:111
  82.8 4.3 %copy.101 = bf16[128,64,128]{2,1,0:T(8,128)(2,1)} copy(bf16[128,64,128]{2,0,1:T(8,128)(2,1)} %fusion.20) | data formatting | bytes 4194304 | tf_op jit(solution)/shard_map/optimization_barrier | solution.py:201
  87.1 4.9 %all-to-all-start.2 = ((bf16[128,64,128]{2,1,0:T(8,128)(2,1)}), bf16[128,64,128]{2,1,0:T(8,128)(2,1)}, u32[]{:S(2)}, u32[]{:S(2)}) async-start(bf16[128,64,128]{2,1,0:T(8,128)(2,1)} %copy.101), calls=%async_computation.2 | async-start | bytes 4194304 | tf_op jit(solution)/shard_map/all_to_all | solution.py:111
  92.0 2.4 convert_reduce_fusion
  94.4 2.5 fusion.4
  97.0 1.6 convolution_convert_fusion.2
  100.0 2.0 copy.104.refs_4_
  102.0 3.7 %fusion.23.refs_2_ = bf16[8,64,512]{2,1,0:T(8,128)(2,1)} fusion(bf16[8,512,256]{2,1,0:T(8,128)(2,1)} %param.18, f32[8,512]{1,0:T(8,128)S(1)} %add_rsqrt_fusion.2, f32[8,512]{1,0:T(8,128)S(1)} %broadcast_multiply_fusion.2, bf16[256,64]{0,1:T(8,128)(2,1)S(1)} %copy-done.18), kind=kOutput, calls=%fused_computation.39 | convolution fusion | flops 138674176 | bytes 2686976 | tf_op jit(solution)/shard_map/snc,ce->sen/dot_general | solution.py:25
  105.6 3.5 %fusion.24.refs_3_ = bf16[8,64,512]{2,1,0:T(8,128)(2,1)} fusion(bf16[8,512,256]{2,1,0:T(8,128)(2,1)} %param.18, f32[8,512]{1,0:T(8,128)S(1)} %add_rsqrt_fusion.2, f32[8,512]{1,0:T(8,128)S(1)} %broadcast_multiply_fusion.2, bf16[256,64]{0,1:T(8,128)(2,1)S(1)} %copy-done.19), kind=kOutput, calls=%fused_computation.40 | convolution fusion | flops 138674176 | bytes 2686976 | tf_op jit(solution)/shard_map/snc,ce->sen/dot_general | solution.py:25
  109.2 2.3 fusion.25.refs_0_
  111.5 4.1 %copy.102 = f32[512,2,512]{0,2,1:T(8,128)} copy(f32[512,2,512]{2,1,0:T(2,128)} %all-gather.2.cloned.1.call-done) | data formatting | bytes 4194304 | tf_op jit(solution)/shard_map/optimization_barrier | solution.py:201
  115.6 15.7 %attention.1 = bf16[8,64,512]{2,1,0:T(8,128)(2,1)} custom-call(bf16[8,64,512]{2,1,0:T(8,128)(2,1)} %fusion.25.refs_0_, bf16[8,512,64]{2,1,0:T(8,128)(2,1)} %copy.103.refs_1_, bf16[8,64,512]{2,1,0:T(8,128)(2,1)} %fusion.23.refs_2_, bf16[8,64,512]{2,1,0:T(8,128)(2,1)} %fusion.24.refs_3_, f32[8,512,1]{2,1,0:T(8,128)} %copy.104.refs_4_, f32[2,512,512]{2,1,0:T(8,128)} %bitcast.69), custom_call_target="tpu_custom_call" | custom-call | flops 4294967296 | bytes 4718592 | tf_op jit(solution)/shard_map/attention/pallas_call | solution.py:55
  131.3 4.2 %collective-permute-start = (bf16[8,64,512]{2,1,0:T(8,128)(2,1)}, bf16[8,64,512]{2,1,0:T(8,128)(2,1)S(1)}, u32[]{:S(2)}, u32[]{:S(2)}) collective-permute-start(bf16[8,64,512]{2,1,0:T(8,128)(2,1)} %attention.1), channel_id=1, source_target_pairs={{0,1},{1,2},{2,3},{4,5},{5,6},{6,7},{8,9},{9,10},{10,11},{12,13},{... | collective-permute-start | bytes 1572872 | tf_op jit(solution)/shard_map/ppermute | solution.py:118
  136.8 9.7 %collective-permute-done = bf16[8,64,512]{2,1,0:T(8,128)(2,1)S(1)} collective-permute-done((bf16[8,64,512]{2,1,0:T(8,128)(2,1)}, bf16[8,64,512]{2,1,0:T(8,128)(2,1)S(1)}, u32[]{:S(2)}, u32[]{:S(2)}) %collective-permute-start) | collective-permute-done | bytes 524320 | tf_op jit(solution)/shard_map/ppermute | solution.py:118
  146.5 4.2 %collective-permute-done.1 = bf16[8,64,512]{2,1,0:T(8,128)(2,1)S(1)} collective-permute-done((bf16[8,64,512]{2,1,0:T(8,128)(2,1)}, bf16[8,64,512]{2,1,0:T(8,128)(2,1)S(1)}, u32[]{:S(2)}, u32[]{:S(2)}) %collective-permute-start.1) | collective-permute-done | bytes 524320 | tf_op jit(solution)/shard_map/ppermute | solution.py:118
  150.7 5.1 %triangle.1 = bf16[8,4,4,64,128]{4,3,2,1,0:T(8,128)(2,1)} custom-call(bf16[8,4,4,64,128]{4,3,2,1,0:T(8,128)(2,1)} %bitcast.11.left_ref, bf16[8,4,4,64,128]{4,3,2,1,0:T(8,128)(2,1)} %bitcast.12.right_ref), custom_call_target="tpu_custom_call" | custom-call | flops 2147483648 | bytes 6291456 | tf_op jit(solution)/shard_map/triangle/pallas_call | solution.py:97
  155.7 4.6 %all-to-all-start.3 = ((bf16[128,64,128]{2,1,0:T(8,128)(2,1)}), bf16[128,64,128]{2,1,0:T(8,128)(2,1)}, u32[]{:S(2)}, u32[]{:S(2)}) async-start(bf16[128,64,128]{2,1,0:T(8,128)(2,1)} %bitcast.68), calls=%async_computation.3 | async-start | bytes 4194304 | tf_op jit(solution)/shard_map/all_to_all | solution.py:111
  163.1 45.9 %collective-permute-done.2 = bf16[8,64,512]{2,1,0:T(8,128)(2,1)} collective-permute-done((bf16[8,64,512]{2,1,0:T(8,128)(2,1)S(1)}, bf16[8,64,512]{2,1,0:T(8,128)(2,1)}, u32[]{:S(2)}, u32[]{:S(2)}) %collective-permute-start.2) | collective-permute-done | bytes 524320 | tf_op jit(solution)/shard_map/ppermute | solution.py:118
  213.3 20.9 %collective-permute-done.3 = bf16[8,64,512]{2,1,0:T(8,128)(2,1)} collective-permute-done((bf16[8,64,512]{2,1,0:T(8,128)(2,1)}, bf16[8,64,512]{2,1,0:T(8,128)(2,1)}, u32[]{:S(2)}, u32[]{:S(2)}) %collective-permute-start.3) | collective-permute-done | bytes 524320 | tf_op jit(solution)/shard_map/ppermute | solution.py:118
  236.7 2.1 fusion.8
  238.7 2.0 convert_reduce_fusion.1
  240.7 2.2 fusion.6
  242.9 2.3 fusion.7
  245.2 1.6 fusion.17
  247.4 2.9 %add_convert_fusion = bf16[64,128,128]{1,2,0:T(8,128)(2,1)} fusion(f32[64,128,128]{1,2,0:T(8,128)S(1)} %copy-done.3, f32[64,128,128]{1,2,0:T(8,128)S(1)} %fusion.17, bf16[64,128,128]{1,2,0:T(8,128)(2,1)S(1)} %multiply_convert_fusion.2, bf16[128,128]{1,0:T(8,128)(2,1)S(1)} %copy-done.21), kind=kOutput, calls=%fused_computation.16 | convolution fusion | flops 274726912 | bytes 12615680 | tf_op jit(solution)/shard_map/ijc,ce->ije/dot_general | solution.py:25
  250.3 4.1 %copy.110 = bf16[64,128,128]{2,1,0:T(8,128)(2,1)} copy(bf16[64,128,128]{1,2,0:T(8,128)(2,1)} %add_convert_fusion) | data formatting | bytes 4194304
  (87 shorter events, 23.4 us)
Async XLA Ops:
  7.2 16.2 %copy-start = (bf16[128,128]{1,0:T(8,128)(2,1)S(1)}, bf16[128,128]{1,0:T(8,128)(2,1)}, u32[]{:S(2)}) copy-start(bf16[128,128]{1,0:T(8,128)(2,1)} %param.30) | copy-start | bytes 98308
  7.2 4.8 %copy-start.10 = (bf16[66,128]{1,0:T(8,128)(2,1)S(1)}, bf16[66,128]{1,0:T(8,128)(2,1)}, u32[]{:S(2)}) copy-start(bf16[66,128]{1,0:T(8,128)(2,1)} %param.23) | copy-start | bytes 50692
  13.8 1.9 copy-start.2
  14.6 8.6 %copy-start.12 = (s32[512]{0:T(512)S(1)}, s32[512]{0:T(512)}, u32[]{:S(2)}) copy-start(s32[512]{0:T(512)} %param.20) | copy-start | bytes 6148
  16.1 8.1 %copy-start.15 = (bf16[128,128]{1,0:T(8,128)(2,1)S(1)}, bf16[128,128]{1,0:T(8,128)(2,1)}, u32[]{:S(2)}) copy-start(bf16[128,128]{1,0:T(8,128)(2,1)} %param.31) | copy-start | bytes 98308
  16.8 15.3 %all-to-all-start = ((f32[64,8,128]{2,0,1:T(8,128)}), f32[64,8,128]{2,0,1:T(8,128)S(1)}, u32[]{:S(2)}, u32[]{:S(2)}) async-start(f32[64,8,128]{2,0,1:T(8,128)} %copy.94), calls=%async_computation | async-start | bytes 524288 | tf_op jit(solution)/shard_map/all_to_all | solution.py:177
  25.7 11.3 %copy-start.8 = (bf16[128,128]{1,0:T(8,128)(2,1)S(1)}, bf16[128,128]{1,0:T(8,128)(2,1)}, u32[]{:S(2)}) copy-start(bf16[128,128]{1,0:T(8,128)(2,1)} %param.32) | copy-start | bytes 98308
  32.1 50.7 %all-to-all-start.1 = ((bf16[128,64,128]{2,1,0:T(8,128)(2,1)}), bf16[128,64,128]{2,1,0:T(8,128)(2,1)}, u32[]{:S(2)}, u32[]{:S(2)}) async-start(bf16[128,64,128]{2,1,0:T(8,128)(2,1)} %copy.100), calls=%async_computation.1 | async-start | bytes 4194304 | tf_op jit(solution)/shard_map/all_to_all | solution.py:111
  35.9 1.9 copy-start.16
  35.9 46.9 %all-gather.2.cloned.1.call-start = ((), (), s32[]{:S(2)}) async-start(), calls=%async_computation.4 | async-start | bytes 2359296 | tf_op jit(solution)/shard_map/all_gather | solution.py:185
  87.1 9.9 %copy-start.17 = (bf16[256,64]{0,1:T(8,128)(2,1)S(1)}, bf16[256,64]{0,1:T(8,128)(2,1)}, u32[]{:S(2)}) copy-start(bf16[256,64]{0,1:T(8,128)(2,1)} %param.26) | copy-start | bytes 98308
  87.1 63.5 %all-to-all-start.2 = ((bf16[128,64,128]{2,1,0:T(8,128)(2,1)}), bf16[128,64,128]{2,1,0:T(8,128)(2,1)}, u32[]{:S(2)}, u32[]{:S(2)}) async-start(bf16[128,64,128]{2,1,0:T(8,128)(2,1)} %copy.101), calls=%async_computation.2 | async-start | bytes 4194304 | tf_op jit(solution)/shard_map/all_to_all | solution.py:111
  92.0 5.0 %copy-start.4 = (bf16[8,512,256]{2,1,0:T(8,128)(2,1)S(1)}, bf16[8,512,256]{2,1,0:T(8,128)(2,1)}, u32[]{:S(2)}) copy-start(bf16[8,512,256]{2,1,0:T(8,128)(2,1)} %param.18) | copy-start | bytes 6291460
  94.4 5.6 %copy-start.11 = (s32[8,512]{1,0:T(8,128)S(1)}, s32[8,512]{1,0:T(8,128)}, u32[]{:S(2)}) copy-start(s32[8,512]{1,0:T(8,128)} %param.19) | copy-start | bytes 49156
  96.9 5.0 %copy-start.18 = (bf16[256,64]{0,1:T(8,128)(2,1)S(1)}, bf16[256,64]{0,1:T(8,128)(2,1)}, u32[]{:S(2)}) copy-start(bf16[256,64]{0,1:T(8,128)(2,1)} %param.27) | copy-start | bytes 98308
  98.6 7.0 %copy-start.19 = (bf16[256,64]{0,1:T(8,128)(2,1)S(1)}, bf16[256,64]{0,1:T(8,128)(2,1)}, u32[]{:S(2)}) copy-start(bf16[256,64]{0,1:T(8,128)(2,1)} %param.28) | copy-start | bytes 98308
  102.0 7.2 %copy-start.5 = (bf16[8,512,256]{2,1,0:T(8,128)(2,1)S(1)}, bf16[8,512,256]{2,1,0:T(8,128)(2,1)}, u32[]{:S(2)}) copy-start(bf16[8,512,256]{2,1,0:T(8,128)(2,1)} %param.18) | copy-start | bytes 6291460
  102.0 7.2 %copy-start.20 = (bf16[256,64]{0,1:T(8,128)(2,1)S(1)}, bf16[256,64]{0,1:T(8,128)(2,1)}, u32[]{:S(2)}) copy-start(bf16[256,64]{0,1:T(8,128)(2,1)} %param.25) | copy-start | bytes 98308
  131.3 15.2 %collective-permute-start = (bf16[8,64,512]{2,1,0:T(8,128)(2,1)}, bf16[8,64,512]{2,1,0:T(8,128)(2,1)S(1)}, u32[]{:S(2)}, u32[]{:S(2)}) collective-permute-start(bf16[8,64,512]{2,1,0:T(8,128)(2,1)} %attention.1), channel_id=1, source_target_pairs={{0,1},{1,2},{2,3},{4,5},{5,6},{6,7},{8,9},{9,10},{10,11},{12,13},{... | collective-permute-start | bytes 1572872 | tf_op jit(solution)/shard_map/ppermute | solution.py:118
  135.5 15.2 %collective-permute-start.1 = (bf16[8,64,512]{2,1,0:T(8,128)(2,1)}, bf16[8,64,512]{2,1,0:T(8,128)(2,1)S(1)}, u32[]{:S(2)}, u32[]{:S(2)}) collective-permute-start(bf16[8,64,512]{2,1,0:T(8,128)(2,1)} %attention.1), channel_id=1, source_target_pairs={{1,0},{2,1},{3,2},{5,4},{6,5},{7,6},{9,8},{10,9},{11,10},{13,12},{... | collective-permute-start | bytes 1572872 | tf_op jit(solution)/shard_map/ppermute | solution.py:118
  150.7 61.1 %copy-start.7 = (bf16[256,256]{1,0:T(8,128)(2,1)S(1)}, bf16[256,256]{1,0:T(8,128)(2,1)}, u32[]{:S(2)}) copy-start(bf16[256,256]{1,0:T(8,128)(2,1)} %param.29) | copy-start | bytes 393220
  155.7 83.0 %all-to-all-start.3 = ((bf16[128,64,128]{2,1,0:T(8,128)(2,1)}), bf16[128,64,128]{2,1,0:T(8,128)(2,1)}, u32[]{:S(2)}, u32[]{:S(2)}) async-start(bf16[128,64,128]{2,1,0:T(8,128)(2,1)} %bitcast.68), calls=%async_computation.3 | async-start | bytes 4194304 | tf_op jit(solution)/shard_map/all_to_all | solution.py:111
  160.4 48.7 %collective-permute-start.2 = (bf16[8,64,512]{2,1,0:T(8,128)(2,1)S(1)}, bf16[8,64,512]{2,1,0:T(8,128)(2,1)}, u32[]{:S(2)}, u32[]{:S(2)}) collective-permute-start(bf16[8,64,512]{2,1,0:T(8,128)(2,1)S(1)} %collective-permute-done.1), channel_id=1, source_target_pairs={{1,0},{2,1},{5,4},{6,5},{9,8},{10,9},{13,12},{14,13},{17,16},{18,1... | collective-permute-start | bytes 1572872 | tf_op jit(solution)/shard_map/ppermute | solution.py:118
  161.7 48.7 %collective-permute-start.4 = (bf16[8,64,512]{2,1,0:T(8,128)(2,1)S(1)}, bf16[8,64,512]{2,1,0:T(8,128)(2,1)}, u32[]{:S(2)}, u32[]{:S(2)}) collective-permute-start(bf16[8,64,512]{2,1,0:T(8,128)(2,1)S(1)} %collective-permute-done), channel_id=1, source_target_pairs={{1,2},{2,3},{5,6},{6,7},{9,10},{10,11},{13,14},{14,15},{17,18},{18... | collective-permute-start | bytes 1572872 | tf_op jit(solution)/shard_map/ppermute | solution.py:118
  209.0 25.2 %collective-permute-start.3 = (bf16[8,64,512]{2,1,0:T(8,128)(2,1)}, bf16[8,64,512]{2,1,0:T(8,128)(2,1)}, u32[]{:S(2)}, u32[]{:S(2)}) collective-permute-start(bf16[8,64,512]{2,1,0:T(8,128)(2,1)} %collective-permute-done.2), channel_id=1, source_target_pairs={{1,0},{5,4},{9,8},{13,12},{17,16},{21,20},{25,24},{29,28}} | collective-permute-start | bytes 1572872 | tf_op jit(solution)/shard_map/ppermute | solution.py:118
  210.3 25.1 %collective-permute-start.5 = (bf16[8,64,512]{2,1,0:T(8,128)(2,1)}, bf16[8,64,512]{2,1,0:T(8,128)(2,1)}, u32[]{:S(2)}, u32[]{:S(2)}) collective-permute-start(bf16[8,64,512]{2,1,0:T(8,128)(2,1)} %collective-permute-done.4), channel_id=1, source_target_pairs={{2,3},{6,7},{10,11},{14,15},{18,19},{22,23},{26,27},{30,31}} | collective-permute-start | bytes 1572872 | tf_op jit(solution)/shard_map/ppermute | solution.py:118
  211.8 24.8 %copy-start.6 = (bf16[8,512,256]{2,1,0:T(8,128)(2,1)S(1)}, bf16[8,512,256]{2,1,0:T(8,128)(2,1)}, u32[]{:S(2)}) copy-start(bf16[8,512,256]{2,1,0:T(8,128)(2,1)} %param.18) | copy-start | bytes 6291460
  211.8 24.8 %copy-start.14 = (bf16[8,64,512]{2,1,0:T(8,128)(2,1)S(1)}, bf16[8,64,512]{2,1,0:T(8,128)(2,1)}, u32[]{:S(2)}) copy-start(bf16[8,64,512]{2,1,0:T(8,128)(2,1)} %attention.1) | copy-start | bytes 1572868
  238.7 6.4 %copy-start.9 = (bf16[128,128]{1,0:T(8,128)(2,1)S(1)}, bf16[128,128]{1,0:T(8,128)(2,1)}, u32[]{:S(2)}) copy-start(bf16[128,128]{1,0:T(8,128)(2,1)} %param.35) | copy-start | bytes 98308
  245.2 2.2 copy-start.3
  245.2 2.2 copy-start.21
  247.4 7.0 %copy-start.1 = (bf16[128,128]{1,0:T(8,128)(2,1)S(1)}, bf16[128,128]{1,0:T(8,128)(2,1)}, u32[]{:S(2)}) copy-start(bf16[128,128]{1,0:T(8,128)(2,1)} %param.30) | copy-start | bytes 98308
  (1 other events, 1.1 us)
Sparse Core Ops, SparseCore 0:
  38.6 36.7 all-gather.1
